TPU v7x, 128 devices: a whole 4x4x4 slice. The times are simulated.
128 devices in a mesh: data: 1, inner: 64 (over z, y, x), stage: 2 (over core).
Axes of the slice: x: 4, y: 4, z: 4, core: 2. Of those that a mesh axis runs over, the one named last changes fastest.
Arguments:
- x: bfloat16 [16, 4096, 1024], P(('data', 'stage'), 'inner')
- g: bfloat16 [16, 4096, 1024], P(('data', 'stage'), 'inner')
- w1: bfloat16 [1, 2, 1024, 4096], P(None, 'stage')
- w2: bfloat16 [1, 2, 4096, 1024], P(None, 'stage')
Outputs:
- output 1: bfloat16 [16, 4096, 1024], P(('data', 'stage'), 'inner')
- output 2: bfloat16 [16, 4096, 1024], P(('data', 'stage'), 'inner')
- output 3: float32 [1, 2, 1024, 4096], P('data', 'stage')
- output 4: float32 [1, 2, 4096, 1024], P('data', 'stage')
All inputs are finite; a program needn't handle non-finite values.
Results may differ from a plain program's by a relative error of at most 0.00491169.
Values are sent between devices in bfloat16 or wider.
A program may use at most 1 GiB of HBM per device.

v0:
```python
import jax
import jax.numpy as jnp
from jax import lax
from jax.sharding import PartitionSpec as P


def _gelu(t):
    return jax.nn.gelu(t, approximate=True)


def _fwd(h, w1, w2):
    z = jnp.dot(h, w1, preferred_element_type=jnp.float32)
    a = _gelu(z).astype(jnp.bfloat16)
    u = jnp.dot(a, w2, preferred_element_type=jnp.float32)
    return (h.astype(jnp.float32) + u).astype(jnp.bfloat16)


def _bwd(h, dh, w1, w2):
    z = jnp.dot(h, w1, preferred_element_type=jnp.float32)
    a32, gelu_vjp = jax.vjp(_gelu, z)
    a = a32.astype(jnp.bfloat16)
    dw2 = jnp.dot(a.T, dh, preferred_element_type=jnp.float32)
    da = jnp.dot(dh, w2.T, preferred_element_type=jnp.float32)
    dz = gelu_vjp(da)[0].astype(jnp.bfloat16)
    dw1 = jnp.dot(h.T, dz, preferred_element_type=jnp.float32)
    dh_prev = (dh.astype(jnp.float32) + jnp.dot(dz, w1.T, preferred_element_type=jnp.float32)).astype(jnp.bfloat16)
    return dh_prev, dw1, dw2


def solution(mesh):
    n_stage = mesh.shape["stage"]
    fwd_perm = [(i, (i + 1) % n_stage) for i in range(n_stage)]
    bwd_perm = [(i, (i - 1) % n_stage) for i in range(n_stage)]

    def body(x, g, w1, w2):
        p = lax.axis_index("stage")
        q = n_stage - 1 - p
        nv, k, d, f = w1.shape
        mb, bl, _ = x.shape
        m = mb * n_stage
        n_ticks = nv * m + n_stage - 1
        x_all = lax.all_gather(x, "stage", axis=0, tiled=True)
        g_all = lax.all_gather(g, "stage", axis=0, tiled=True)

        def slot(s):
            valid = (s >= 0) & (s < nv * m)
            sc = jnp.clip(s, 0, nv * m - 1)
            return valid, sc // m, sc % m

        def fwd_tick(carry, t):
            inc, buf, saved, y_all = carry
            ok_in, _, m_in = slot(t - n_stage)
            buf = buf.at[m_in].set(jnp.where(ok_in & (p == 0), inc, buf[m_in]))
            ok, v, mi = slot(t - p)
            h = jnp.where(p == 0, jnp.where(v == 0, x_all[mi], buf[mi]), inc)
            w1v, w2v = w1[v], w2[v]
            hs = []
            for j in range(k):
                hs.append(h)
                h = _fwd(h, w1v[j], w2v[j])
            saved = saved.at[v, mi].set(jnp.where(ok, jnp.stack(hs), saved[v, mi]))
            last = ok & (p == n_stage - 1) & (v == nv - 1)
            y_all = y_all.at[mi].set(jnp.where(last, h, y_all[mi]))
            inc = lax.ppermute(h, "stage", fwd_perm)
            return (inc, buf, saved, y_all), None

        act0 = jnp.zeros((bl, d), jnp.bfloat16)
        per_mb0 = jnp.zeros((m, bl, d), jnp.bfloat16)
        saved0 = jnp.zeros((nv, m, k, bl, d), jnp.bfloat16)
        ticks = jnp.arange(n_ticks, dtype=jnp.int32)
        (_, _, saved, y_all), _ = lax.scan(fwd_tick, (act0, per_mb0, saved0, per_mb0), ticks)

        def bwd_tick(carry, t):
            inc, buf, dw1, dw2, dx_all = carry
            ok_in, _, m_in = slot(t - n_stage)
            buf = buf.at[m_in].set(jnp.where(ok_in & (q == 0), inc, buf[m_in]))
            ok, u, mi = slot(t - q)
            v = nv - 1 - u
            dh = jnp.where(q == 0, jnp.where(u == 0, g_all[mi], buf[mi]), inc)
            hs = saved[v, mi]
            w1v, w2v = w1[v], w2[v]
            d1s = [None] * k
            d2s = [None] * k
            for j in reversed(range(k)):
                dh, d1s[j], d2s[j] = _bwd(hs[j], dh, w1v[j], w2v[j])
            on = ok.astype(jnp.float32)
            dw1 = dw1.at[v].add(jnp.stack(d1s) * on)
            dw2 = dw2.at[v].add(jnp.stack(d2s) * on)
            first = ok & (p == 0) & (v == 0)
            dx_all = dx_all.at[mi].set(jnp.where(first, dh, dx_all[mi]))
            inc = lax.ppermute(dh, "stage", bwd_perm)
            return (inc, buf, dw1, dw2, dx_all), None

        dw1_0 = jnp.zeros((nv, k, d, f), jnp.float32)
        dw2_0 = jnp.zeros((nv, k, f, d), jnp.float32)
        (_, _, dw1, dw2, dx_all), _ = lax.scan(bwd_tick, (act0, per_mb0, dw1_0, dw2_0, per_mb0), ticks)

        zero = jnp.zeros_like(y_all)
        y = lax.psum_scatter(jnp.where(p == n_stage - 1, y_all, zero), "stage", scatter_dimension=0, tiled=True)
        dx = lax.psum_scatter(jnp.where(p == 0, dx_all, zero), "stage", scatter_dimension=0, tiled=True)
        dw1 = lax.psum(dw1, "inner")
        dw2 = lax.psum(dw2, "inner")
        return y, dx, dw1, dw2

    tok = P(("data", "stage"), "inner", None)
    wsp = P(None, "stage", None, None)
    dsp = P("data", "stage", None, None)
    return jax.shard_map(body, mesh=mesh, in_specs=(tok, tok, wsp, wsp), out_specs=(tok, tok, dsp, dsp), check_vma=False)
```

profile of v0, /device:TPU:0, one launch (start us, length us, event | category | flops | bytes accessed | tf_op | source)
XLA Modules:
  0.0 1492.5 jit_solution(11298563442281332919)
XLA Ops:
  8.7 16.7 %all-gather.3.cloned.1.call-done = bf16[16,64,1024]{2,1,0:T(8,128)(2,1)} async-done(((bf16[8,64,1024]{2,1,0:T(8,128)(2,1)}), bf16[16,64,1024]{2,1,0:T(8,128)(2,1)}) %all-gather.3.cloned.1.call-update) | async-done | bytes 2097168 | tf_op jit(solution)/shard_map/all_gather | solution.py:42
  29.0 333.6 %while.46 = (s32[]{:T(128)}, bf16[64,1024]{1,0:T(8,128)(2,1)S(1)}, bf16[16,64,1024]{2,1,0:T(8,128)(2,1)}, bf16[1,16,1,64,1024]{4,3,2,1,0:T(8,128)(2,1)}, bf16[16...) while((s32[]{:T(128)}, bf16[64,1024]{1,0:T(8,128)(2,1)S(1)}, ...), condition=%wide.region_4.5_spmd, body=%wide.region_0.4_spmd.sunk | while | flops 1076822144 | bytes 19926796 | solution.py:71
  367.6 736.1 %while.47 = (s32[]{:T(128)}, bf16[64,1024]{1,0:T(8,128)(2,1)S(1)}, bf16[16,64,1024]{2,1,0:T(8,128)(2,1)}, f32[1,1,1024,4096]{3,2,1,0:T(8,128)}, f32[1,1,4096,102...) while((s32[]{:T(128)}, bf16[64,1024]{1,0:T(8,128)(2,1)S(1)}, ...), condition=%wide.region_10.11_spmd.clone, body=%wide.region_6.10_spmd.clone.sunk | while | flops 2726100992 | bytes 158733136 | solution.py:96
  426.0 11.6 add_select_fusion.5
  469.7 11.6 add_select_fusion.5
  481.3 11.4 add_select_fusion.4
  513.3 11.6 add_select_fusion.5
  557.0 11.6 add_select_fusion.5
  600.6 11.6 add_select_fusion.5
  644.2 11.6 add_select_fusion.5
  687.9 11.6 add_select_fusion.5
  731.5 11.6 add_select_fusion.5
  775.2 11.6 add_select_fusion.5
  818.8 11.6 add_select_fusion.5
  862.5 11.6 add_select_fusion.5
  874.1 11.4 add_select_fusion.4
  906.1 11.6 add_select_fusion.5
  949.8 11.6 add_select_fusion.5
  993.3 11.6 add_select_fusion.5
  1037.1 11.6 add_select_fusion.5
  1080.6 11.6 add_select_fusion.5
  1107.4 12.7 reduce-scatter.5.cloned.1.call-done
  1120.1 343.2 %all-reduce.3.cloned.1.call-done = (f32[1,1,1024,4096]{3,2,1,0:T(8,128)}, f32[1,1,4096,1024]{3,2,1,0:T(8,128)}) async-done(((f32[1,1,1024,4096]{3,2,1,0:T(8,128)}, f32[1,1,4096,1024]{3,2,1,0:T(8,128)}), (f32[1,1,1024,4096]{3,2,1,0:T(8,128)}, f32[1,1,4096,1024]{3,2,1,0:T(8,128)})) %all-reduce.3.cloned.1.call-update) | async-done | bytes 33554448 | tf_op jit(solution)/shard_map/psum | solution.py:101
  1463.4 12.6 copy.48
  (541 shorter events, 840.0 us)
Async XLA Ops:
  7.2 18.3 %all-gather.3.cloned.1.call-start = ((), (), s32[]{:S(2)}) async-start(), calls=%async_computation.2 | async-start | bytes 3145728 | tf_op jit(solution)/shard_map/all_gather | solution.py:42
  7.9 356.5 %all-gather.5.cloned.1.call-start = ((), (), s32[]{:S(2)}) async-start(), calls=%async_computation.4 | async-start | bytes 3145728 | tf_op jit(solution)/shard_map/all_gather | solution.py:43
  8.6 1098.8 %reduce-scatter.3.cloned.1.call-start = ((), (), s32[]{:S(2)}) async-start(), calls=%async_computation.3 | async-start | bytes 3145728 | tf_op jit(solution)/shard_map/reduce_scatter | solution.py:99
  47.2 1.4 collective-permute-start
  66.8 1.4 collective-permute-start
  364.1 756.0 %reduce-scatter.5.cloned.1.call-start = ((), (), s32[]{:S(2)}) async-start(), calls=%async_computation.5 | async-start | bytes 3145728 | tf_op jit(solution)/shard_map/reduce_scatter | solution.py:100
  387.2 18.2 %collective-permute-start.1 = (bf16[64,1024]{1,0:T(8,128)(2,1)S(1)}, bf16[64,1024]{1,0:T(8,128)(2,1)S(1)}, u32[]{:S(2)}, u32[]{:S(2)}) collective-permute-start(bf16[64,1024]{1,0:T(8,128)(2,1)S(1)} %get-tuple-element.707), channel_id=1, source_target_pairs={{0,1},{1,0},{2,3},{3,2},{4,5},{5,4},{6,7},{7,6},{8,9},{9,8},{10,11... | collective-permute-start | bytes 393224 | tf_op jit(solution)/shard_map/while/body/eval_jaxpr/ppermute | solution.py:91
  425.0 24.0 %collective-permute-start.1 = (bf16[64,1024]{1,0:T(8,128)(2,1)S(1)}, bf16[64,1024]{1,0:T(8,128)(2,1)S(1)}, u32[]{:S(2)}, u32[]{:S(2)}) collective-permute-start(bf16[64,1024]{1,0:T(8,128)(2,1)S(1)} %get-tuple-element.707), channel_id=1, source_target_pairs={{0,1},{1,0},{2,3},{3,2},{4,5},{5,4},{6,7},{7,6},{8,9},{9,8},{10,11... | collective-permute-start | bytes 393224 | tf_op jit(solution)/shard_map/while/body/eval_jaxpr/ppermute | solution.py:91
  468.7 24.0 %collective-permute-start.1 = (bf16[64,1024]{1,0:T(8,128)(2,1)S(1)}, bf16[64,1024]{1,0:T(8,128)(2,1)S(1)}, u32[]{:S(2)}, u32[]{:S(2)}) collective-permute-start(bf16[64,1024]{1,0:T(8,128)(2,1)S(1)} %get-tuple-element.707), channel_id=1, source_target_pairs={{0,1},{1,0},{2,3},{3,2},{4,5},{5,4},{6,7},{7,6},{8,9},{9,8},{10,11... | collective-permute-start | bytes 393224 | tf_op jit(solution)/shard_map/while/body/eval_jaxpr/ppermute | solution.py:91
  512.3 24.0 %collective-permute-start.1 = (bf16[64,1024]{1,0:T(8,128)(2,1)S(1)}, bf16[64,1024]{1,0:T(8,128)(2,1)S(1)}, u32[]{:S(2)}, u32[]{:S(2)}) collective-permute-start(bf16[64,1024]{1,0:T(8,128)(2,1)S(1)} %get-tuple-element.707), channel_id=1, source_target_pairs={{0,1},{1,0},{2,3},{3,2},{4,5},{5,4},{6,7},{7,6},{8,9},{9,8},{10,11... | collective-permute-start | bytes 393224 | tf_op jit(solution)/shard_map/while/body/eval_jaxpr/ppermute | solution.py:91
  556.0 24.0 %collective-permute-start.1 = (bf16[64,1024]{1,0:T(8,128)(2,1)S(1)}, bf16[64,1024]{1,0:T(8,128)(2,1)S(1)}, u32[]{:S(2)}, u32[]{:S(2)}) collective-permute-start(bf16[64,1024]{1,0:T(8,128)(2,1)S(1)} %get-tuple-element.707), channel_id=1, source_target_pairs={{0,1},{1,0},{2,3},{3,2},{4,5},{5,4},{6,7},{7,6},{8,9},{9,8},{10,11... | collective-permute-start | bytes 393224 | tf_op jit(solution)/shard_map/while/body/eval_jaxpr/ppermute | solution.py:91
  599.6 24.0 %collective-permute-start.1 = (bf16[64,1024]{1,0:T(8,128)(2,1)S(1)}, bf16[64,1024]{1,0:T(8,128)(2,1)S(1)}, u32[]{:S(2)}, u32[]{:S(2)}) collective-permute-start(bf16[64,1024]{1,0:T(8,128)(2,1)S(1)} %get-tuple-element.707), channel_id=1, source_target_pairs={{0,1},{1,0},{2,3},{3,2},{4,5},{5,4},{6,7},{7,6},{8,9},{9,8},{10,11... | collective-permute-start | bytes 393224 | tf_op jit(solution)/shard_map/while/body/eval_jaxpr/ppermute | solution.py:91
  643.3 24.0 %collective-permute-start.1 = (bf16[64,1024]{1,0:T(8,128)(2,1)S(1)}, bf16[64,1024]{1,0:T(8,128)(2,1)S(1)}, u32[]{:S(2)}, u32[]{:S(2)}) collective-permute-start(bf16[64,1024]{1,0:T(8,128)(2,1)S(1)} %get-tuple-element.707), channel_id=1, source_target_pairs={{0,1},{1,0},{2,3},{3,2},{4,5},{5,4},{6,7},{7,6},{8,9},{9,8},{10,11... | collective-permute-start | bytes 393224 | tf_op jit(solution)/shard_map/while/body/eval_jaxpr/ppermute | solution.py:91
  686.9 24.0 %collective-permute-start.1 = (bf16[64,1024]{1,0:T(8,128)(2,1)S(1)}, bf16[64,1024]{1,0:T(8,128)(2,1)S(1)}, u32[]{:S(2)}, u32[]{:S(2)}) collective-permute-start(bf16[64,1024]{1,0:T(8,128)(2,1)S(1)} %get-tuple-element.707), channel_id=1, source_target_pairs={{0,1},{1,0},{2,3},{3,2},{4,5},{5,4},{6,7},{7,6},{8,9},{9,8},{10,11... | collective-permute-start | bytes 393224 | tf_op jit(solution)/shard_map/while/body/eval_jaxpr/ppermute | solution.py:91
  730.5 24.0 %collective-permute-start.1 = (bf16[64,1024]{1,0:T(8,128)(2,1)S(1)}, bf16[64,1024]{1,0:T(8,128)(2,1)S(1)}, u32[]{:S(2)}, u32[]{:S(2)}) collective-permute-start(bf16[64,1024]{1,0:T(8,128)(2,1)S(1)} %get-tuple-element.707), channel_id=1, source_target_pairs={{0,1},{1,0},{2,3},{3,2},{4,5},{5,4},{6,7},{7,6},{8,9},{9,8},{10,11... | collective-permute-start | bytes 393224 | tf_op jit(solution)/shard_map/while/body/eval_jaxpr/ppermute | solution.py:91
  774.2 24.0 %collective-permute-start.1 = (bf16[64,1024]{1,0:T(8,128)(2,1)S(1)}, bf16[64,1024]{1,0:T(8,128)(2,1)S(1)}, u32[]{:S(2)}, u32[]{:S(2)}) collective-permute-start(bf16[64,1024]{1,0:T(8,128)(2,1)S(1)} %get-tuple-element.707), channel_id=1, source_target_pairs={{0,1},{1,0},{2,3},{3,2},{4,5},{5,4},{6,7},{7,6},{8,9},{9,8},{10,11... | collective-permute-start | bytes 393224 | tf_op jit(solution)/shard_map/while/body/eval_jaxpr/ppermute | solution.py:91
  817.9 24.0 %collective-permute-start.1 = (bf16[64,1024]{1,0:T(8,128)(2,1)S(1)}, bf16[64,1024]{1,0:T(8,128)(2,1)S(1)}, u32[]{:S(2)}, u32[]{:S(2)}) collective-permute-start(bf16[64,1024]{1,0:T(8,128)(2,1)S(1)} %get-tuple-element.707), channel_id=1, source_target_pairs={{0,1},{1,0},{2,3},{3,2},{4,5},{5,4},{6,7},{7,6},{8,9},{9,8},{10,11... | collective-permute-start | bytes 393224 | tf_op jit(solution)/shard_map/while/body/eval_jaxpr/ppermute | solution.py:91
  861.5 24.0 %collective-permute-start.1 = (bf16[64,1024]{1,0:T(8,128)(2,1)S(1)}, bf16[64,1024]{1,0:T(8,128)(2,1)S(1)}, u32[]{:S(2)}, u32[]{:S(2)}) collective-permute-start(bf16[64,1024]{1,0:T(8,128)(2,1)S(1)} %get-tuple-element.707), channel_id=1, source_target_pairs={{0,1},{1,0},{2,3},{3,2},{4,5},{5,4},{6,7},{7,6},{8,9},{9,8},{10,11... | collective-permute-start | bytes 393224 | tf_op jit(solution)/shard_map/while/body/eval_jaxpr/ppermute | solution.py:91
  905.2 24.0 %collective-permute-start.1 = (bf16[64,1024]{1,0:T(8,128)(2,1)S(1)}, bf16[64,1024]{1,0:T(8,128)(2,1)S(1)}, u32[]{:S(2)}, u32[]{:S(2)}) collective-permute-start(bf16[64,1024]{1,0:T(8,128)(2,1)S(1)} %get-tuple-element.707), channel_id=1, source_target_pairs={{0,1},{1,0},{2,3},{3,2},{4,5},{5,4},{6,7},{7,6},{8,9},{9,8},{10,11... | collective-permute-start | bytes 393224 | tf_op jit(solution)/shard_map/while/body/eval_jaxpr/ppermute | solution.py:91
  948.8 24.1 %collective-permute-start.1 = (bf16[64,1024]{1,0:T(8,128)(2,1)S(1)}, bf16[64,1024]{1,0:T(8,128)(2,1)S(1)}, u32[]{:S(2)}, u32[]{:S(2)}) collective-permute-start(bf16[64,1024]{1,0:T(8,128)(2,1)S(1)} %get-tuple-element.707), channel_id=1, source_target_pairs={{0,1},{1,0},{2,3},{3,2},{4,5},{5,4},{6,7},{7,6},{8,9},{9,8},{10,11... | collective-permute-start | bytes 393224 | tf_op jit(solution)/shard_map/while/body/eval_jaxpr/ppermute | solution.py:91
  992.5 23.9 %collective-permute-start.1 = (bf16[64,1024]{1,0:T(8,128)(2,1)S(1)}, bf16[64,1024]{1,0:T(8,128)(2,1)S(1)}, u32[]{:S(2)}, u32[]{:S(2)}) collective-permute-start(bf16[64,1024]{1,0:T(8,128)(2,1)S(1)} %get-tuple-element.707), channel_id=1, source_target_pairs={{0,1},{1,0},{2,3},{3,2},{4,5},{5,4},{6,7},{7,6},{8,9},{9,8},{10,11... | collective-permute-start | bytes 393224 | tf_op jit(solution)/shard_map/while/body/eval_jaxpr/ppermute | solution.py:91
  1036.0 24.1 %collective-permute-start.1 = (bf16[64,1024]{1,0:T(8,128)(2,1)S(1)}, bf16[64,1024]{1,0:T(8,128)(2,1)S(1)}, u32[]{:S(2)}, u32[]{:S(2)}) collective-permute-start(bf16[64,1024]{1,0:T(8,128)(2,1)S(1)} %get-tuple-element.707), channel_id=1, source_target_pairs={{0,1},{1,0},{2,3},{3,2},{4,5},{5,4},{6,7},{7,6},{8,9},{9,8},{10,11... | collective-permute-start | bytes 393224 | tf_op jit(solution)/shard_map/while/body/eval_jaxpr/ppermute | solution.py:91
  1079.7 23.9 %collective-permute-start.1 = (bf16[64,1024]{1,0:T(8,128)(2,1)S(1)}, bf16[64,1024]{1,0:T(8,128)(2,1)S(1)}, u32[]{:S(2)}, u32[]{:S(2)}) collective-permute-start(bf16[64,1024]{1,0:T(8,128)(2,1)S(1)} %get-tuple-element.707), channel_id=1, source_target_pairs={{0,1},{1,0},{2,3},{3,2},{4,5},{5,4},{6,7},{7,6},{8,9},{9,8},{10,11... | collective-permute-start | bytes 393224 | tf_op jit(solution)/shard_map/while/body/eval_jaxpr/ppermute | solution.py:91
  1106.8 356.6 %all-reduce.3.cloned.1.call-start = ((), (), s32[]{:S(2)}) async-start(), calls=%async_computation.6 | async-start | bytes 67108864 | tf_op jit(solution)/shard_map/psum | solution.py:101
  (69 other events, 435.3 us)
Sparse Core Ops, SparseCore 0:
  9.6 15.7 all-gather.2
  27.1 14.6 all-gather.4
  364.2 13.1 reduce-scatter.2
  1106.9 13.1 reduce-scatter.4
  1126.7 336.6 all-reduce.2
where the time goes:
time: 1500 us; the launch traced here: 1490 us
  matrix products  755 us (50%)
  waiting for transfers between devices  393 us (26%)
  other arithmetic  168 us (11%)
  local copies, waits for them, and re-layouts  109 us (7%)
  loops' own time  44.3 us (3%)
    psum x1, waiting for transfers between devices, body(): dw1 = lax.psum(dw1, 'inner')  343 us
    dot_general x17, matrix products, _bwd(): dw2 = jnp.dot(a.T, dh, preferred_element_type=jnp.float32)  195 us
    dot_general x17, matrix products, _bwd(): dw1 = jnp.dot(h.T, dz, preferred_element_type=jnp.float32)  191 us
    dot_general x17, matrix products, _fwd(): u = jnp.dot(a, w2, preferred_element_type=jnp.float32)  163 us
    dot_general x17, matrix products, _bwd(): z = jnp.dot(h, w1, preferred_element_type=jnp.float32)  89.4 us
    dot_general x17, matrix products, _bwd(): jnp.dot(dz, w1.T, preferred_element_type=jnp.float32)  67.1 us
    dot_general x17, matrix products, _bwd(): da = jnp.dot(dh, w2.T, preferred_element_type=jnp.float32)  48.8 us
    another operation x68, other arithmetic  48 us
  transfers between devices with their start and end apart: 39, of which 20 were waited for; matrix products, arithmetic and copies ran while one was open for 67% of the time, Pallas kernels for 0%

commit v1 on v0

v1 whole, which is shorter than its diff:
```python
import functools

import jax
import jax.numpy as jnp
from jax import lax
from jax.experimental import pallas as pl
from jax.experimental.pallas import tpu as pltpu
from jax.sharding import PartitionSpec as P

MESH = pl.DeviceIdType.MESH
F32 = jnp.float32
BF16 = jnp.bfloat16
N = 4
STEPS = 14
OWN = 6
FAR = 4

_K = 0.7978845608028654
_C = 0.044715


def _gelu_and_slope(z):
    z2 = z * z
    t = jnp.tanh(z * (_K + (_K * _C) * z2))
    cdf = 0.5 + 0.5 * t
    slope = cdf + (z * (1.0 - t * t)) * (0.5 * _K + (1.5 * _K * _C) * z2)
    return z * cdf, slope


def _dot(a, b, dims=((1,), (0,))):
    return lax.dot_general(a, b, (dims, ((), ())), preferred_element_type=F32)


def _ds(start, size):
    return pl.ds(pl.multiple_of(start, size), size)


def _kernel(
    RB, F,
    x_ref, g_ref, w1_ref, w2_ref,
    y_ref, dx_ref, o1_ref, o2_ref, spill_ref,
    w1, w2, LT, R, hv, BUF, ST, Z, YS,
    SA1, HA1, SB1, HB1, RR1,
    SA2, HA2, SB2, HB2, RR2,
    SA3, HA3, SB3, HB3,
    AG,
    ld_sem, xg_send, xg_recv, ex_send, ex_recv, sp_w, sp_r, out_send, out_recv, out_loc,
    msend, mrecv, own_sem, near_sem, opp_sem,
):
    D = 4 * RB
    CW = RB
    HW = CW // 2
    TU = 2 * RB
    FT = F // 8
    n2 = (F // D) * (D // CW)
    n_parts = n2 + F // CW
    NQ = (n_parts + 2) // 3
    NT = NQ + STEPS - 1
    rows = (RB, RB // 4, RB // 16)

    st = lax.axis_index("stage")
    me = lax.axis_index("inner")
    c = (me % N, (me // N) % N, me // (N * N))
    stride = (1, N, N * N)

    def at(dim, delta):
        return (c[dim] + delta) % N

    nbr = [
        tuple(me + (at(dim, delta) - c[dim]) * stride[dim] for delta in (1, -1))
        for dim in range(3)
    ]

    def remote(src, dst, ss, rs, to, core):
        return pltpu.make_async_remote_copy(
            src_ref=src, dst_ref=dst, send_sem=ss, recv_sem=rs, device_id=(0, to, core), device_id_type=MESH
        )

    def await_(ref, sem):
        pltpu.make_async_copy(ref, ref, sem).wait()

    partner = 1 - st

    own_rows = _ds(st * TU, TU)
    lw1 = pltpu.make_async_copy(w1_ref, w1, ld_sem.at[0])
    lw2 = pltpu.make_async_copy(w2_ref, w2, ld_sem.at[1])

    barrier = pltpu.get_barrier_semaphore()
    pl.semaphore_signal(barrier, inc=1, device_id=(0, me, partner), device_id_type=MESH)
    for dim in range(3):
        for to in nbr[dim]:
            pl.semaphore_signal(barrier, inc=1, device_id=(0, to, st), device_id_type=MESH)

    @pl.when(st == 0)
    def _():
        pltpu.make_async_copy(x_ref, hv.at[own_rows, :], ld_sem.at[2]).start()
        lw1.start()
        lw2.start()

    @pl.when(st == 1)
    def _():
        pltpu.make_async_copy(g_ref, R.at[own_rows, pl.ds(0, D)], ld_sem.at[2]).start()
        lw2.start()
        lw1.start()

    pl.semaphore_wait(barrier, 7)

    def x_over():
        return remote(x_ref, hv.at[own_rows, :], xg_send, xg_recv, me, partner)

    def g_over():
        return remote(g_ref, R.at[own_rows, pl.ds(0, D)], xg_send, xg_recv, me, partner)

    def spill_w(k):
        return pltpu.make_async_copy(ST.at[k % 2], spill_ref.at[k], sp_w.at[k % 2])

    def spill_r(k):
        return pltpu.make_async_copy(spill_ref.at[k], ST.at[k % 2], sp_r.at[k % 2])

    def urows(u):
        return _ds(u * TU, TU)

    def h_transposed(u):
        @pl.loop(0, 4)
        def _(k):
            LT[_ds(F + k * RB, RB), urows(u)] = hv[urows(u), _ds(k * RB, RB)].T

    def put_a(u, j, a):
        LT[_ds(j * FT, FT), urows(u)] = a.T

    def put_dz(u, j, dz):
        R[urows(u), _ds(D + j * FT, FT)] = dz

    def z_tile(u, j):
        return _dot(hv[urows(u), :], w1[:, _ds(j * FT, FT)])

    def da_tile(u, j):
        return _dot(R[urows(u), pl.ds(0, D)], w2[_ds(j * FT, FT), :], ((1,), (1,)))

    def dh_tile(u, ct):
        acc = _dot(R[urows(u), pl.ds(D, F)], w1[_ds(ct * RB, RB), :], ((1,), (1,)))
        return (R[urows(u), _ds(ct * RB, RB)].astype(F32) + acc).astype(BF16)

    def across(u, ct, val, dst):
        for r in range(2):
            SB1[ct * 2 + r] = val[r * RB : (r + 1) * RB]
        for r in range(2):
            remote(
                SB1.at[ct * 2 + r], dst.at[_ds(u * TU + r * RB, RB), _ds(ct * RB, RB)],
                ex_send.at[u], ex_recv.at[u], me, partner,
            ).start()

    def across_sent(u):
        await_(SB1.at[pl.ds(0, 8)], ex_send.at[u])

    @pl.when(st == 0)
    def _():
        g_over().start()
        pltpu.make_async_copy(x_ref, hv.at[own_rows, :], ld_sem.at[2]).wait()
        lw1.wait()

        @pl.loop(0, 2)
        def _(u):
            @pl.when(u == 1)
            def _():
                await_(hv.at[pl.ds(0, TU), :], xg_recv)

            Z[0] = z_tile(u, 0)
            h_transposed(u)

            def finish(j, z):
                a, slope = _gelu_and_slope(z)
                a = a.astype(BF16)
                for r in range(2):
                    for k in range(FT // CW):
                        BUF[r * (F // CW) + j * (FT // CW) + k] = a[r * RB : (r + 1) * RB, k * CW : (k + 1) * CW]
                put_a(u, j, a)
                return slope

            def spill(j, slope):
                k = u * 8 + j
                ST[k % 2] = slope
                spill_w(k).start()

            @pl.loop(0, 7)
            def _(j):
                @pl.when(u * 8 + j >= 2)
                def _():
                    spill_w(u * 8 + j).wait()

                Z[(j + 1) % 2] = z_tile(u, j + 1)
                spill(j, finish(j, Z[j % 2]))

            spill_w(u * 8 + 7).wait()
            spill(7, finish(7, Z[1]))

            @pl.when(u == 0)
            def _():
                lw2.wait()

            @pl.when(u == 1)
            def _():
                across_sent(0)

            @pl.loop(0, 4)
            def _(ct):
                a = jnp.concatenate(
                    [jnp.concatenate([BUF[r * (F // CW) + k] for k in range(F // CW)], axis=1) for r in range(2)], axis=0
                )
                acc = _dot(a, w2[:, _ds(ct * RB, RB)])
                h1 = (hv[urows(u), _ds(ct * RB, RB)].astype(F32) + acc).astype(BF16)
                across(u, ct, h1, hv)

        spill_w(0).wait()
        spill_w(1).wait()
        across_sent(1)
        g_over().wait_send()
        spill_r(0).start()

        @pl.loop(0, 2)
        def _(u):
            await_(SB1.at[pl.ds(0, 8)], ex_recv.at[u])
            Z[0] = da_tile(u, 0)

            def finish(k, j, da):
                spill_r(k).wait()
                put_dz(u, j, (da * ST[k % 2]).astype(BF16))

            @pl.loop(0, 7)
            def _(j):
                k = u * 8 + j
                spill_r(k + 1).start()
                Z[(j + 1) % 2] = da_tile(u, j + 1)
                finish(k, j, Z[j % 2])

            @pl.when(u == 0)
            def _():
                spill_r(8).start()

            finish(u * 8 + 7, 7, Z[1])

    @pl.when(st == 1)
    def _():
        x_over().start()
        pltpu.make_async_copy(g_ref, R.at[own_rows, pl.ds(0, D)], ld_sem.at[2]).wait()
        lw2.wait()

        @pl.loop(0, 2)
        def _(i):
            @pl.when(i == 1)
            def _():
                await_(hv.at[pl.ds(0, TU), :], xg_recv)

            @pl.loop(0, 8)
            def _(j):
                k = (1 - i) * 8 + j

                @pl.when(i * 8 + j >= 2)
                def _():
                    spill_w(k).wait()

                ST[k % 2] = da_tile(1 - i, j)
                spill_w(k).start()

        spill_w(0).wait()
        spill_w(1).wait()
        lw1.wait()
        x_over().wait_send()
        spill_r(0).start()

        @pl.loop(0, 2)
        def _(u):
            await_(SB1.at[pl.ds(0, 8)], ex_recv.at[u])
            Z[0] = z_tile(u, 0)
            h_transposed(u)

            def finish(k, j, z):
                spill_r(k).wait()
                a, slope = _gelu_and_slope(z)
                put_a(u, j, a.astype(BF16))
                put_dz(u, j, (ST[k % 2] * slope).astype(BF16))

            @pl.loop(0, 7)
            def _(j):
                k = u * 8 + j
                spill_r(k + 1).start()
                Z[(j + 1) % 2] = z_tile(u, j + 1)
                finish(k, j, Z[j % 2])

            @pl.when(u == 0)
            def _():
                spill_r(8).start()

            finish(u * 8 + 7, 7, Z[1])

            @pl.when(u == 1)
            def _():
                across_sent(0)

            @pl.loop(0, 4)
            def _(ct):
                across(u, ct, dh_tile(u, ct), R)

        across_sent(1)

    def out_tile(k):
        u, ct, s = k // 4, k % 4, k % 2

        def to(ref, local):
            dst = ref.at[:, _ds(ct * RB, RB)]
            if local:
                return pltpu.make_async_copy(YS.at[s], dst, out_loc.at[s])
            return remote(YS.at[s], dst, out_send.at[s], out_recv, me, partner)

        def sent(k):
            @pl.when(k // 4 == st)
            def _():
                await_(YS.at[s], out_loc.at[s])

            @pl.when(k // 4 != st)
            def _():
                await_(YS.at[s], out_send.at[s])

        @pl.when(k >= 2)
        def _():
            sent(k - 2)

        @pl.when(k < 8)
        def _():
            @pl.when(st == 0)
            def _():
                YS[s] = dh_tile(u, ct)

                @pl.when(u == 0)
                def _():
                    to(dx_ref, True).start()

                @pl.when(u == 1)
                def _():
                    to(dx_ref, False).start()

            @pl.when(st == 1)
            def _():
                acc = _dot(LT[pl.ds(0, F), urows(u)], w2[:, _ds(ct * RB, RB)], ((0,), (0,)))
                YS[s] = (hv[urows(u), _ds(ct * RB, RB)].astype(F32) + acc).astype(BF16)

                @pl.when(u == 0)
                def _():
                    to(y_ref, False).start()

                @pl.when(u == 1)
                def _():
                    to(y_ref, True).start()

    def axis(j, level):
        return (j + level) % 3

    def part(q, j):
        return jnp.minimum(3 * q + j, n_parts - 1)

    def lrow(n, r):
        return jnp.where(n < n2, (n // 4) * D + r * RB, F + r * RB)

    def rcol(n):
        return jnp.where(n < n2, (n % 4) * CW, D + (n - n2) * CW)

    def product(q, j, r):
        n = part(q, j)
        return _dot(LT[_ds(lrow(n, r), RB), :], R[:, _ds(rcol(n), CW)])

    def send(kind, q, j, level, way, src, dst):
        s = q % 2
        remote(src, dst, msend.at[kind, s], mrecv.at[kind, s], nbr[axis(j, level)][way], st).start()

    def came(kind, q, ref):
        await_(ref, mrecv.at[kind, q % 2])

    def gone(kind, q, ref):
        await_(ref, msend.at[kind, q % 2])

    SA, HA, SB, HB = (SA1, SA2, SA3), (HA1, HA2, HA3), (SB1, SB2, SB3), (HB1, HB2, HB3)
    RR = (None, RR1, RR2)

    def sb(level, q, j, way):
        return SB[level].at[((q % 2) * 3 + j) * 2 + way]

    def block(level, q, j, delta):
        r = at(axis(j, level), delta)
        if level == 0:
            return product(q, j, r)
        return RR[level][q % 2, j, _ds(r * rows[level], rows[level]), :]

    def first(level, q):
        for j in range(3):
            SA[level][q % 2, j] = block(level, q, j, 2).astype(BF16)
        for j in range(3):
            for way in range(2):
                send(
                    2 * level, q, j, level, way,
                    SA[level].at[q % 2, j, :, pl.ds(way * HW, HW)], HA[level].at[q % 2, j, way],
                )

    def second(level, q):
        s = q % 2
        came(2 * level, q, HA[level].at[s])
        for j in range(3):
            for way in range(2):
                own = block(level, q, j, 1 - 2 * way)
                here = own[:, way * HW : (way + 1) * HW] + HA[level][s, j, way].astype(F32)
                there = own[:, (1 - way) * HW : (2 - way) * HW]
                halves = (here, there) if way == 0 else (there, here)
                SB[level][(s * 3 + j) * 2 + way] = jnp.concatenate(halves, axis=1).astype(BF16)
        for j in range(3):
            for way in range(2):
                send(2 * level + 1, q, j, level, way, sb(level, q, j, way), HB[level].at[s, j, way])
        gone(2 * level, q, SA[level].at[s])

    def third(level, q):
        s = q % 2
        came(2 * level + 1, q, HB[level].at[s])
        total = [
            block(level, q, j, 0) + (HB[level][s, j, 0].astype(F32) + HB[level][s, j, 1].astype(F32)) for j in range(3)
        ]
        gone(2 * level + 1, q, HB[level].at[s])
        return total

    def own(q, j, level, delta, half=None):
        a = at(axis(j, 1), delta if level == 1 else 0) * rows[1]
        if level == 2:
            a = a + at(axis(j, 2), delta) * rows[2]
        cols = slice(None) if half is None else pl.ds(half * HW, HW)
        return AG.at[q % OWN, j, _ds(a, rows[level]), cols]

    def span(k):
        return AG.at[0, :, pl.ds(0, k), :]

    def near(q, j, pos, half=None):
        k = ((q % FAR) * 3 + j) * 3 + pos
        return BUF.at[k] if half is None else BUF.at[k, :, pl.ds(half * HW, HW)]

    def out_copy(q, j, src, delta, sem):
        n = part(q, j)
        r = at(axis(j, 0), delta)

        @pl.when(3 * q + j < n2)
        def _():
            pltpu.make_async_copy(src, o2_ref.at[_ds((n // 4) * D + r * RB, RB), _ds((n % 4) * CW, CW)], sem).start()

        @pl.when((3 * q + j >= n2) & (3 * q + j < n_parts))
        def _():
            pltpu.make_async_copy(src, o1_ref.at[_ds(r * RB, RB), _ds((n - n2) * CW, CW)], sem).start()

    def out_done(q, j, blocks, sem):
        @pl.when(3 * q + j < n_parts)
        def _():
            await_(BUF.at[pl.ds(0, blocks)], sem)

    def s1(q):
        first(0, q)

    def s2(q):
        second(0, q)

    def s3(q):
        for j, total in enumerate(third(0, q)):
            RR1[q % 2, j] = total
        first(1, q)

    def s4(q):
        second(1, q)

    def s5(q):
        for j, total in enumerate(third(1, q)):
            RR2[q % 2, j] = total
        first(2, q)

    def s6(q):
        second(2, q)

    def s7(q):
        for j, total in enumerate(third(2, q)):
            a = at(axis(j, 1), 0) * rows[1] + at(axis(j, 2), 0) * rows[2]
            AG[q % OWN, j, _ds(a, rows[2]), :] = total.astype(BF16)
        for j in range(3):
            for way in range(2):
                send(6, q, j, 2, way, own(q, j, 2, 0), own(q, j, 2, 0))

    def s8(q):
        came(6, q, span(2 * rows[2]))
        gone(6, q, span(2 * rows[2]))
        for j in range(3):
            for way in range(2):
                blk = own(q, j, 2, 2 * way - 1, way)
                send(7, q, j, 2, way, blk, blk)

    def s9(q):
        came(7, q, span(rows[2]))
        gone(7, q, span(rows[2]))
        for j in range(3):
            for way in range(2):
                send(8, q, j, 1, way, own(q, j, 1, 0), own(q, j, 1, 0))

    def s10(q):
        came(8, q, span(2 * rows[1]))
        gone(8, q, span(2 * rows[1]))
        for j in range(3):
            for way in range(2):
                blk = own(q, j, 1, 2 * way - 1, way)
                send(9, q, j, 1, way, blk, blk)

    def s11(q):
        came(9, q, span(rows[1]))
        gone(9, q, span(rows[1]))
        for j in range(3):
            for way in range(2):
                send(10, q, j, 0, way, AG.at[q % OWN, j], near(q, j, way))
        for j in range(3):
            out_copy(q, j, AG.at[q % OWN, j], 0, own_sem.at[q % 2])

    def s12(q):
        came(10, q, BUF.at[pl.ds(0, 6)])
        gone(10, q, BUF.at[pl.ds(0, 6)])
        for j in range(3):
            for way in range(2):
                send(11, q, j, 0, way, near(q, j, way, way), near(q, j, 2, way))
        for j in range(3):
            out_done(q, j, 1, own_sem.at[q % 2])
            for way in range(2):
                out_copy(q, j, near(q, j, way), 2 * way - 1, near_sem.at[q % 2])

    def s13(q):
        came(11, q, BUF.at[pl.ds(0, 3)])
        gone(11, q, BUF.at[pl.ds(0, 3)])
        for j in range(3):
            out_done(q, j, 2, near_sem.at[q % 2])
            out_copy(q, j, near(q, j, 2), 2, opp_sem.at[q % 2])

    def s14(q):
        for j in range(3):
            out_done(q, j, 1, opp_sem.at[q % 2])

    steps = (s1, s2, s3, s4, s5, s6, s7, s8, s9, s10, s11, s12, s13, s14)

    @pl.loop(0, NT)
    def _(t):
        for k in reversed(range(STEPS)):
            q = t - k

            @pl.when((q >= 0) & (q < NQ))
            def _():
                steps[k](q)

        k = t - 6

        @pl.when((k >= 0) & (k < 10))
        def _():
            out_tile(k)

    await_(BUF.at[pl.ds(0, 8)], out_recv)


def _one(x, g, w1, w2):
    T2, D = x.shape
    F = w1.shape[1]
    RB = D // 4
    V, S = pltpu.VMEM, pltpu.SemaphoreType
    rows = (RB, RB // 4, RB // 16)

    def ring(level):
        r = rows[level]
        return [
            V((2, 3, r, RB), BF16),
            V((2, 3, 2, r, RB // 2), BF16),
            V((12, r, RB), BF16),
            V((2, 3, 2, r, RB), BF16),
        ]

    scratch = [
        V((D, F), BF16),
        V((F, D), BF16),
        V((F + D, 2 * T2), BF16),
        V((2 * T2, D + F), BF16),
        V((2 * T2, D), BF16),
        V((9 * FAR, RB, RB), BF16),
        V((2, T2, F // 8), F32),
        V((2, T2, F // 8), F32),
        V((2, T2, RB), BF16),
        *ring(0),
        V((2, 3, RB, RB), F32),
        *ring(1),
        V((2, 3, RB // 4, RB), F32),
        *ring(2),
        V((OWN, 3, RB, RB), BF16),
        S.DMA((3,)),
        S.DMA,
        S.DMA,
        S.DMA((2,)),
        S.DMA((2,)),
        S.DMA((2,)),
        S.DMA((2,)),
        S.DMA((2,)),
        S.DMA,
        S.DMA((2,)),
        S.DMA((12, 2)),
        S.DMA((12, 2)),
        S.DMA((2,)),
        S.DMA((2,)),
        S.DMA((2,)),
    ]
    hbm = pl.BlockSpec(memory_space=pl.ANY)
    sds = jax.ShapeDtypeStruct
    return pl.pallas_call(
        functools.partial(_kernel, RB, F),
        name="mlp_stack",
        out_shape=[
            sds((T2, D), BF16),
            sds((T2, D), BF16),
            sds((D, F), BF16),
            sds((F, D), BF16),
            sds((16, T2, F // 8), F32),
        ],
        in_specs=[hbm] * 4,
        out_specs=[hbm] * 5,
        scratch_shapes=scratch,
        compiler_params=pltpu.CompilerParams(
            collective_id=0, has_side_effects=True, vmem_limit_bytes=67_043_328
        ),
    )(x, g, w1, w2)


def solution(mesh):
    def body(x, g, w1, w2):
        mb, bl, d = x.shape
        f = w1.shape[-1]
        y, dx, dw1, dw2, _ = _one(x.reshape(mb * bl, d), g.reshape(mb * bl, d), w1.reshape(d, f), w2.reshape(f, d))
        return (
            y.reshape(x.shape),
            dx.reshape(x.shape),
            dw1.astype(F32).reshape(1, 1, d, f),
            dw2.astype(F32).reshape(1, 1, f, d),
        )

    tok = P(("data", "stage"), "inner", None)
    wsp = P(None, "stage", None, None)
    dsp = P("data", "stage", None, None)
    return jax.shard_map(body, mesh=mesh, in_specs=(tok, tok, wsp, wsp), out_specs=(tok, tok, dsp, dsp), check_vma=False)
```

time: 1500 us -> 247 us (0.16)
  matrix products: 755 us -> 0 us
  waiting for transfers between devices: 393 us -> 0 us
  Pallas kernels: 0 us -> 220 us
  other arithmetic: 168 us -> 23.7 us
  local copies, waits for them, and re-layouts: 109 us -> 1.95 us
  loops' own time: 44.3 us -> 0 us
    dot_general x102 -> x0, matrix products: 755 us -> none  [the longest x17 195 us: _bwd(): dw2 = jnp.dot(a.T, dh, preferred_element_type=jnp.float32)]
    psum x1 -> x0, waiting for transfers between devices: 343 us -> none  [body(): dw1 = lax.psum(dw1, 'inner')]
    pallas_call x0 -> x1, Pallas kernels: none -> 220 us  [_one(): pl.pallas_call(functools.partial(_kernel, RB, F), name='mlp_stack', out_s...]
    scatter x51 -> x0, other arithmetic: 98.2 us -> none  [the longest x17 39.4 us: fwd_tick(): saved = saved.at[v, mi].set(jnp.where(ok, jnp.stack(hs), saved[v, mi]))]
    dynamic_slice x85 -> x0, local copies, waits for them, and re-layouts: 69 us -> none  [the longest x34 19.7 us: body(): lax.scan(fwd_tick, (act0, per_mb0, saved0, per_mb0), ticks)]
    another operation x68 -> x0, other arithmetic: 48 us -> none
    another operation x2 -> x0, loops' own time: 44.3 us -> none  [the longest x1 24.1 us: body(): lax.scan(bwd_tick, (act0, per_mb0, dw1_0, dw2_0, per_mb0), ticks)]
    reshape x0 -> x2, other arithmetic: none -> 23.7 us  [the longest x1 11.8 us: body(): dw2.astype(F32).reshape(1, 1, f, d)]
  transfers between devices with their start and end apart: 39 -> 0, of which waited for: 20 -> 0; matrix products, arithmetic and copies ran while one was open for 67% -> 0% of each run, Pallas kernels for 0% -> 0%
where the time goes in v1:
time: 247 us; the launch traced here: 246 us
  Pallas kernels  220 us (89%)
  other arithmetic  23.7 us (10%)
    pallas_call x1, Pallas kernels, _one(): pl.pallas_call(functools.partial(_kernel, RB, F), name='mlp_stack', out_s...  220 us
    reshape x1, other arithmetic, body(): dw2.astype(F32).reshape(1, 1, f, d)  11.8 us
    reshape x1, other arithmetic, body(): dw1.astype(F32).reshape(1, 1, d, f)  11.8 us

profile of v1, /device:TPU:0, one launch (start us, length us, event | category | flops | bytes accessed | tf_op | source)
XLA Modules:
  0.0 246.2 jit_solution(16394146801906980129)
XLA Ops:
  0.6 220.0 %mlp_stack.1 = (bf16[512,1024]{1,0:T(8,128)(2,1)}, bf16[512,1024]{1,0:T(8,128)(2,1)}, bf16[1024,4096]{1,0:T(8,128)(2,1)}, bf16[4096,1024]{1,0:T(8,128)(2,1)}, f32[16,512,512]{2,1,0:T(8,128)}) custom-call(bf16[512,1024]{1,0:T(8,128)(2,1)} %bitcast.14, bf16[512,1024]{1,0:T(8,128)(2,1)} %bitcast.15, bf16[1024,4096]{1,0:T(8,128)(2,1)} %bitcast.12, ...), custom_call_target="tpu_custom_call" | custom-call | tf_op jit(solution)/shard_map/mlp_stack/pallas_call | solution.py:612
  220.6 11.8 %bitcast_convert_fusion.1 = f32[1,1,1024,4096]{3,2,1,0:T(8,128)} fusion(bf16[1024,4096]{1,0:T(8,128)(2,1)} %get-tuple-element.10), kind=kLoop, calls=%fused_computation.1 | loop fusion | flops 4194304 | bytes 25165824 | tf_op jit(solution)/shard_map/reshape | solution.py:639
  232.4 0.0 copy-start.1
  232.4 0.0 copy-start
  232.4 11.8 %bitcast_convert_fusion = f32[1,1,4096,1024]{3,2,1,0:T(8,128)} fusion(bf16[4096,1024]{1,0:T(8,128)(2,1)} %get-tuple-element.11), kind=kLoop, calls=%fused_computation | loop fusion | flops 4194304 | bytes 25165824 | tf_op jit(solution)/shard_map/reshape | solution.py:640
  244.3 0.0 copy-done.1
  244.3 1.0 copy.10
  245.2 0.0 copy-done
  245.2 1.0 copy.11
Async XLA Ops:
  232.4 11.9 %copy-start.1 = (bf16[512,1024]{1,0:T(8,128)(2,1)S(1)}, bf16[512,1024]{1,0:T(8,128)(2,1)}, u32[]{:S(2)}) copy-start(bf16[512,1024]{1,0:T(8,128)(2,1)} %get-tuple-element.8) | copy-start | bytes 3145732
  232.4 12.8 %copy-start = (bf16[512,1024]{1,0:T(8,128)(2,1)S(1)}, bf16[512,1024]{1,0:T(8,128)(2,1)}, u32[]{:S(2)}) copy-start(bf16[512,1024]{1,0:T(8,128)(2,1)} %get-tuple-element.9) | copy-start | bytes 3145732
